TPU v7x, 32 devices: a whole 2x2x4 slice. The times are simulated.
32 devices in a mesh: dp: 4 (over y, core), vocab: 8 (over z, x).
Axes of the slice: x: 2, y: 2, z: 4, core: 2. Of those that a mesh axis runs over, the one named last changes fastest.
Arguments:
- teacher_hidden: bfloat16 [512, 16384], P('dp', 'vocab'), may hold values from -120 to 120
- student_hidden: bfloat16 [512, 4096], P('dp', 'vocab'), may hold values from -120 to 120
- teacher_weight: bfloat16 [16384, 65536], P('dp', 'vocab'), may hold values from -1 to 1
- student_weight: bfloat16 [4096, 65536], P('dp', 'vocab'), may hold values from -1 to 1
Outputs:
- kl: float32 [512], P('dp')
- loss: float32 [], replicated
All inputs are finite; a program needn't handle non-finite values.
Results may differ from a plain program's by a relative error of at most 0.0003.
Values may be sent and summed in bfloat16 or wider, within the bound.
No kernel may reach another device: no remote copies, remote signals or barrier semaphores. Data moves between devices by JAX's collectives and lax.ppermute only.
A program may use at most 256 MiB of HBM per device.

v0:
```python
import jax
import jax.numpy as jnp
from jax import lax
from jax.sharding import PartitionSpec as P


def shards(teacher_hidden, student_hidden, teacher_weight, student_weight):
    teacher_full, student_full = (
        lax.all_gather(teacher_hidden, "vocab", axis=1, tiled=True),
        lax.all_gather(student_hidden, "vocab", axis=1, tiled=True),
    )
    tok_rows = teacher_hidden.shape[0]
    shard_vocab = teacher_weight.shape[1]
    teacher_cols, student_cols = (
        lax.all_to_all(teacher_full, "dp", split_axis=1, concat_axis=0, tiled=True),
        lax.all_to_all(student_full, "dp", split_axis=1, concat_axis=0, tiled=True),
    )
    summed = lax.psum_scatter(
        jnp.concatenate(
            [
                jnp.dot(teacher_cols, teacher_weight, preferred_element_type=jnp.float32),
                jnp.dot(student_cols, student_weight, preferred_element_type=jnp.float32),
            ],
            axis=1,
        ),
        "dp",
        scatter_dimension=0,
        tiled=True,
    )
    teacher_logit = summed[:, :shard_vocab]
    student_logit = summed[:, shard_vocab:]
    teacher_local = jnp.max(teacher_logit, axis=1)
    student_local = jnp.max(student_logit, axis=1)
    teacher_top, student_top = lax.pmax((teacher_local, student_local), "vocab")
    teacher_exp = jnp.exp(teacher_logit - teacher_top[:, None])
    teacher_total, weighted, student_total = lax.psum(
        (
            jnp.sum(teacher_exp, axis=1),
            jnp.sum(teacher_exp * (teacher_logit - student_logit), axis=1),
            jnp.sum(jnp.exp(student_logit - student_top[:, None]), axis=1),
        ),
        "vocab",
    )
    teacher_lse = teacher_top + jnp.log(teacher_total)
    student_lse = student_top + jnp.log(student_total)
    kl = weighted / teacher_total - teacher_lse + student_lse
    group_sum = lax.psum(jnp.sum(kl), "dp")
    loss = group_sum / (tok_rows * lax.axis_size("dp"))
    return (kl, loss)


def solution(mesh):
    in_specs = (P("dp", "vocab"), P("dp", "vocab"), P("dp", "vocab"), P("dp", "vocab"))
    out_specs = (P("dp"), P())
    return jax.shard_map(shards, mesh=mesh, in_specs=in_specs, out_specs=out_specs, check_vma=False)
```

profile of v0, /device:TPU:0, one launch (start us, length us, event | category | flops | bytes accessed | tf_op | source)
XLA Modules:
  0.0 567.2 jit_solution(6716977359885407873)
XLA Ops:
  7.2 0.0 all-gather.5.cloned.1.call-start
  7.2 1.7 copy.8
  8.9 0.0 all-gather.5.cloned.1.call-update
  8.9 0.0 all-gather.3.cloned.1.call-start
  8.9 2.1 copy.6
  11.0 0.0 all-gather.3.cloned.1.call-update
  11.0 42.1 %all-gather.5.cloned.1.call-done = bf16[128,4096]{0,1:T(8,128)(2,1)} async-done(((bf16[128,512]{0,1:T(8,128)(2,1)}), bf16[128,4096]{0,1:T(8,128)(2,1)}) %all-gather.5.cloned.1.call-update) | async-done | bytes 1048592 | tf_op jit(solution)/shard_map/all_gather | solution.py:10
  53.1 17.9 %all_to_all.38 = bf16[128,4,1024]{0,2,1:T(8,128)(2,1)S(1)} all-to-all(bf16[128,4,1024]{0,2,1:T(8,128)(2,1)} %bitcast.13), channel_id=1, replica_groups=mesh['dp'=4,'vocab'=8] {'dp'}, dimensions={1} | all-to-all | bytes 2097152 | tf_op jit(solution)/shard_map/all_to_all | solution.py:16
  71.0 55.8 %all-gather.3.cloned.1.call-done = bf16[128,16384]{0,1:T(8,128)(2,1)} async-done(((bf16[128,2048]{0,1:T(8,128)(2,1)}), bf16[128,16384]{0,1:T(8,128)(2,1)}) %all-gather.3.cloned.1.call-update) | async-done | bytes 4194320 | tf_op jit(solution)/shard_map/all_gather | solution.py:9
  126.8 4.8 all-to-all-start
  131.7 0.0 reduce-scatter.2.cloned.1.call-start
  131.7 0.5 copy.9
  132.2 15.6 %fusion.3 = f32[512,8192]{1,0:T(8,128)} fusion(bf16[512,1024]{1,0:T(8,128)(2,1)S(1)} %bitcast.14, bf16[1024,8192]{1,0:T(8,128)(2,1)} %param.7), kind=kOutput, calls=%fused_computation.10 | convolution fusion | flops 8589934592 | bytes 34603008 | tf_op jit(solution)/shard_map/dot_general | solution.py:22
  147.8 32.0 %all-to-all-done = bf16[128,4,4096]{0,2,1:T(8,128)(2,1)} async-done(((bf16[128,4,4096]{0,2,1:T(8,128)(2,1)}), bf16[128,4,4096]{0,2,1:T(8,128)(2,1)}, u32[]{:S(2)}, u32[]{:S(2)}) %all-to-all-start) | async-done | bytes 4194336 | tf_op jit(solution)/shard_map/all_to_all | solution.py:15
  179.9 6.4 %copy.7 = bf16[4,128,4096]{2,1,0:T(8,128)(2,1)} copy(bf16[4,128,4096]{1,2,0:T(8,128)(2,1)} %bitcast.1) | data formatting | bytes 8388608 | tf_op jit(solution)/shard_map/all_to_all | solution.py:15
  186.3 44.2 %fusion.2 = f32[512,8192]{1,0:T(8,128)} fusion(bf16[512,4096]{1,0:T(8,128)(2,1)} %bitcast.11, bf16[4096,8192]{1,0:T(8,128)(2,1)} %param.6), kind=kOutput, calls=%fused_computation.9 | convolution fusion | flops 34359738368 | bytes 88080384 | tf_op jit(solution)/shard_map/dot_general | solution.py:21
  230.5 22.5 %pad_maximum_fusion = f32[512,16384]{1,0:T(8,128)} fusion(f32[512,8192]{1,0:T(8,128)} %fusion.3, f32[512,8192]{1,0:T(8,128)} %fusion.2), kind=kLoop, calls=%fused_computation | loop fusion | flops 8388608 | bytes 67108864 | tf_op jit(solution)/shard_map/concatenate | solution.py:19
  253.0 0.0 reduce-scatter.2.cloned.1.call-update
  253.0 230.1 %reduce-scatter.2.cloned.1.call-done = f32[128,16384]{1,0:T(8,128)} async-done(((f32[512,16384]{1,0:T(8,128)}), f32[128,16384]{1,0:T(8,128)}) %reduce-scatter.2.cloned.1.call-update) | async-done | bytes 8388624 | tf_op jit(solution)/shard_map/reduce_scatter | solution.py:18
  483.1 2.5 slice_reduce_fusion.1
  485.6 21.5 %pmax.14 = f32[128]{0:T(128)S(1)} all-reduce(f32[128]{0:T(128)S(1)} %slice_reduce_fusion.1), channel_id=1, replica_groups=mesh['dp'=4,'vocab'=8] {'vocab'}, use_global_device_ids=true, to_apply=%region_2.0 | all-reduce | flops 128 | bytes 1024 | tf_op jit(solution)/shard_map/pmax | solution.py:34
  507.1 4.9 multiply_reduce_fusion
  512.0 17.1 %pmax.15 = f32[128]{0:T(128)S(1)} all-reduce(f32[128]{0:T(128)S(1)} %get-tuple-element.4), channel_id=1, replica_groups=mesh['dp'=4,'vocab'=8] {'vocab'}, use_global_device_ids=true, to_apply=%region_8.0 | all-reduce | flops 128 | bytes 1024 | tf_op jit(solution)/shard_map/pmax | solution.py:34
  529.2 2.9 exponential_reduce_fusion
  532.1 19.1 %all-reduce = (f32[128]{0:T(128)S(1)}, f32[128]{0:T(128)S(1)}, f32[128]{0:T(128)S(1)}) all-reduce(f32[128]{0:T(128)S(1)} %exponential_reduce_fusion, f32[128]{0:T(128)S(1)} %get-tuple-element.3, f32[128]{0:T(128)S(1)} %get-tuple-element.2), channel_id=1, replica_groups=mesh['dp'=4,'vocab'=8] {'vocab'}, use_global_device_ids=true, to_apply=%region_10.0 | all-reduce | flops 384 | bytes 3072 | tf_op jit(solution)/shard_map/psum | solution.py:36
  551.2 1.1 fusion.1
  552.3 6.5 %psum.31 = f32[]{:T(128)} all-reduce(f32[]{:T(128)} %get-tuple-element.8), channel_id=1, replica_groups=mesh['dp'=4,'vocab'=8] {'dp'}, use_global_device_ids=true, to_apply=%region_12.0 | all-reduce | flops 1 | bytes 8 | tf_op jit(solution)/shard_map/psum | solution.py:47
Async XLA Ops:
  7.2 46.0 %all-gather.5.cloned.1.call-start = ((), (), s32[]{:S(2)}) async-start(), calls=%async_computation.4 | async-start | bytes 1179648 | tf_op jit(solution)/shard_map/all_gather | solution.py:10
  8.9 117.9 %all-gather.3.cloned.1.call-start = ((), (), s32[]{:S(2)}) async-start(), calls=%async_computation.3 | async-start | bytes 4718592 | tf_op jit(solution)/shard_map/all_gather | solution.py:9
  126.8 53.0 %all-to-all-start = ((bf16[128,4,4096]{0,2,1:T(8,128)(2,1)}), bf16[128,4,4096]{0,2,1:T(8,128)(2,1)}, u32[]{:S(2)}, u32[]{:S(2)}) async-start(bf16[128,4,4096]{0,2,1:T(8,128)(2,1)} %bitcast.10), calls=%async_computation | async-start | bytes 8388608 | tf_op jit(solution)/shard_map/all_to_all | solution.py:15
  131.7 351.5 %reduce-scatter.2.cloned.1.call-start = ((), (), s32[]{:S(2)}) async-start(), calls=%async_computation.5 | async-start | bytes 41943040 | tf_op jit(solution)/shard_map/reduce_scatter | solution.py:18
Sparse Core Ops, SparseCore 0:
  10.1 42.9 all-gather.4
  55.3 71.5 all-gather.2
  253.2 229.9 reduce-scatter.1
where the time goes:
time: 568 us; the launch traced here: 567 us
  waiting for transfers between devices  360 us (63%)
  blocking collectives  82.3 us (14%)
  matrix products  59.8 us (11%)
  other arithmetic  33.9 us (6%)
  between operations  15.5 us (3%)
  local copies, waits for them, and re-layouts  10.7 us (2%)
    reduce_scatter x1, waiting for transfers between devices, shards(): lax.psum_scatter(jnp.concatenate([jnp.dot(teacher_cols, teacher_weight, p...  230 us
    all_gather x1, waiting for transfers between devices, shards(): lax.all_gather(teacher_hidden, 'vocab', axis=1, tiled=True)  55.8 us
    dot_general x1, matrix products, shards(): jnp.dot(teacher_cols, teacher_weight, preferred_element_type=jnp.float32)  44.2 us
    all_gather x1, waiting for transfers between devices, shards(): lax.all_gather(student_hidden, 'vocab', axis=1, tiled=True)  42.1 us
    pmax x2, blocking collectives, shards(): teacher_top, student_top = lax.pmax((teacher_local, student_local), 'vocab')  38.7 us
    all_to_all x1, waiting for transfers between devices, shards(): lax.all_to_all(teacher_full, 'dp', split_axis=1, concat_axis=0, tiled=True)  32 us
    concatenate x1, other arithmetic, shards(): jnp.concatenate([jnp.dot(teacher_cols, teacher_weight, preferred_element_...  22.5 us
    psum x1, blocking collectives, shards(): lax.psum((jnp.sum(teacher_exp, axis=1), jnp.sum(teacher_exp * (teacher_lo...  19.1 us
  transfers between devices with their start and end apart: 4, of which 4 were waited for; matrix products, arithmetic and copies ran while one was open for 3% of the time, Pallas kernels for 0%

commit v1 on v0

--- a/solution.py
+++ b/solution.py
@@ -12,7 +12,12 @@
     tok_rows = teacher_hidden.shape[0]
     shard_vocab = teacher_weight.shape[1]
     teacher_cols, student_cols = (
-        lax.all_to_all(teacher_full, "dp", split_axis=1, concat_axis=0, tiled=True),
+        jnp.concatenate(
+            lax.all_to_all(
+                jnp.stack(jnp.split(teacher_full, lax.axis_size("dp"), axis=1)), "dp", 0, 0
+            ),
+            axis=0,
+        ),
         lax.all_to_all(student_full, "dp", split_axis=1, concat_axis=0, tiled=True),
     )
     summed = lax.psum_scatter(

time: 568 us -> 566 us (level)
  blocking collectives: 82.3 us -> 64.4 us
  waiting for transfers between devices: 360 us -> 377 us
  local copies, waits for them, and re-layouts: 10.7 us -> 4.84 us
    all_to_all x1 -> x0, blocking collectives: 17.9 us -> none  [shards(): lax.all_to_all(student_full, 'dp', split_axis=1, concat_axis=0, tiled=True)]
    all_gather x1, waiting for transfers between devices: 55.8 us -> 70.2 us  [shards(): lax.all_gather(teacher_hidden, 'vocab', axis=1, tiled=True)]
    all_to_all x1 -> x0, local copies, waits for them, and re-layouts: 6.44 us -> none  [shards(): lax.all_to_all(teacher_full, 'dp', split_axis=1, concat_axis=0, tiled=True)]
    all_to_all x1 -> x2, waiting for transfers between devices: 32 us -> 32 us  [the longest x1 32 us: shards(): lax.all_to_all(jnp.stack(jnp.split(teacher_full, lax.axis_size('dp'), axi...]
  transfers between devices with their start and end apart: 4 -> 5, of which waited for: 4 -> 4; matrix products, arithmetic and copies ran while one was open for 3% -> 4% of each run, Pallas kernels for 0% -> 0%
where the time goes in v1:
time: 566 us
  waiting for transfers between devices  377 us (67%)
  blocking collectives  64.4 us (11%)
  matrix products  59.8 us (11%)
  other arithmetic  36.2 us (6%)
  between operations  15.6 us (3%)
  starting transfers between devices  8.49 us (2%)
    reduce_scatter x1, waiting for transfers between devices, shards(): lax.psum_scatter(jnp.concatenate([jnp.dot(teacher_cols, teacher_weight, p...  230 us
    all_gather x1, waiting for transfers between devices, shards(): lax.all_gather(teacher_hidden, 'vocab', axis=1, tiled=True)  70.2 us
    dot_general x1, matrix products, shards(): jnp.dot(teacher_cols, teacher_weight, preferred_element_type=jnp.float32)  44.2 us
    all_gather x1, waiting for transfers between devices, shards(): lax.all_gather(student_hidden, 'vocab', axis=1, tiled=True)  43.5 us
    pmax x2, blocking collectives, shards(): teacher_top, student_top = lax.pmax((teacher_local, student_local), 'vocab')  38.7 us
    all_to_all x1, waiting for transfers between devices, shards(): lax.all_to_all(jnp.stack(jnp.split(teacher_full, lax.axis_size('dp'), axi...  32 us
    concatenate x1, other arithmetic, shards(): jnp.concatenate([jnp.dot(teacher_cols, teacher_weight, preferred_element_...  22.5 us
    psum x1, blocking collectives, shards(): lax.psum((jnp.sum(teacher_exp, axis=1), jnp.sum(teacher_exp * (teacher_lo...  19.1 us
  transfers between devices with their start and end apart: 5, of which 4 were waited for; matrix products, arithmetic and copies ran while one was open for 4% of the time, Pallas kernels for 0%

profile of v1, /device:TPU:0, one launch (start us, length us, event | category | flops | bytes accessed | tf_op | source)
XLA Modules:
  0.0 565.7 jit_solution(4775489921679419433)
XLA Ops:
  7.2 0.0 all-gather.5.cloned.1.call-start
  7.2 1.7 copy.6
  8.9 0.0 all-gather.5.cloned.1.call-update
  8.9 0.0 all-gather.3.cloned.1.call-start
  8.9 0.7 all-gather.3.cloned.1.call-update
  9.6 43.5 %all-gather.5.cloned.1.call-done = bf16[128,4096]{0,1:T(8,128)(2,1)} async-done(((bf16[128,512]{0,1:T(8,128)(2,1)}), bf16[128,4096]{0,1:T(8,128)(2,1)}) %all-gather.5.cloned.1.call-update) | async-done | bytes 1048592 | tf_op jit(solution)/shard_map/all_gather | solution.py:10
  53.1 3.5 all-to-all-start.1
  56.6 70.2 %all-gather.3.cloned.1.call-done = bf16[128,16384]{1,0:T(8,128)(2,1)} async-done(((bf16[128,2048]{1,0:T(8,128)(2,1)}), bf16[128,16384]{1,0:T(8,128)(2,1)}) %all-gather.3.cloned.1.call-update) | async-done | bytes 4194320 | tf_op jit(solution)/shard_map/all_gather | solution.py:9
  126.8 2.7 slice_bitcast_fusion.3
  129.5 2.2 pad_maximum_fusion.1
  131.7 0.0 all-to-all-done.1
  131.7 4.9 all-to-all-start
  136.6 0.0 reduce-scatter.2.cloned.1.call-start
  136.7 0.5 copy.7
  137.2 15.6 %fusion.3 = f32[512,8192]{1,0:T(8,128)} fusion(bf16[512,1024]{1,0:T(8,128)(2,1)S(1)} %bitcast.18, bf16[1024,8192]{1,0:T(8,128)(2,1)} %param.7), kind=kOutput, calls=%fused_computation.15 | convolution fusion | flops 8589934592 | bytes 34603008 | tf_op jit(solution)/shard_map/dot_general | solution.py:27
  152.8 32.0 %all-to-all-done = bf16[4,128,4096]{2,1,0:T(8,128)(2,1)} async-done(((bf16[4,128,4096]{2,1,0:T(8,128)(2,1)}), bf16[4,128,4096]{2,1,0:T(8,128)(2,1)}, u32[]{:S(2)}, u32[]{:S(2)}) %all-to-all-start) | async-done | bytes 4194336 | tf_op jit(solution)/shard_map/all_to_all | solution.py:16
  184.8 44.2 %fusion.2 = f32[512,8192]{1,0:T(8,128)} fusion(bf16[512,4096]{1,0:T(8,128)(2,1)} %bitcast.4, bf16[4096,8192]{1,0:T(8,128)(2,1)} %param.6), kind=kOutput, calls=%fused_computation.14 | convolution fusion | flops 34359738368 | bytes 88080384 | tf_op jit(solution)/shard_map/dot_general | solution.py:26
  229.0 22.5 %pad_maximum_fusion = f32[512,16384]{1,0:T(8,128)} fusion(f32[512,8192]{1,0:T(8,128)} %fusion.3, f32[512,8192]{1,0:T(8,128)} %fusion.2), kind=kLoop, calls=%fused_computation | loop fusion | flops 8388608 | bytes 67108864 | tf_op jit(solution)/shard_map/concatenate | solution.py:24
  251.5 0.0 reduce-scatter.2.cloned.1.call-update
  251.6 230.1 %reduce-scatter.2.cloned.1.call-done = f32[128,16384]{1,0:T(8,128)} async-done(((f32[512,16384]{1,0:T(8,128)}), f32[128,16384]{1,0:T(8,128)}) %reduce-scatter.2.cloned.1.call-update) | async-done | bytes 8388624 | tf_op jit(solution)/shard_map/reduce_scatter | solution.py:23
  481.7 2.5 slice_reduce_fusion.1
  484.1 21.5 %pmax.14 = f32[128]{0:T(128)S(1)} all-reduce(f32[128]{0:T(128)S(1)} %slice_reduce_fusion.1), channel_id=1, replica_groups=mesh['dp'=4,'vocab'=8] {'vocab'}, use_global_device_ids=true, to_apply=%region_2.0 | all-reduce | flops 128 | bytes 1024 | tf_op jit(solution)/shard_map/pmax | solution.py:39
  505.7 4.9 multiply_reduce_fusion
  510.6 17.1 %pmax.15 = f32[128]{0:T(128)S(1)} all-reduce(f32[128]{0:T(128)S(1)} %get-tuple-element.4), channel_id=1, replica_groups=mesh['dp'=4,'vocab'=8] {'vocab'}, use_global_device_ids=true, to_apply=%region_8.0 | all-reduce | flops 128 | bytes 1024 | tf_op jit(solution)/shard_map/pmax | solution.py:39
  527.7 2.9 exponential_reduce_fusion
  530.6 19.1 %all-reduce = (f32[128]{0:T(128)S(1)}, f32[128]{0:T(128)S(1)}, f32[128]{0:T(128)S(1)}) all-reduce(f32[128]{0:T(128)S(1)} %exponential_reduce_fusion, f32[128]{0:T(128)S(1)} %get-tuple-element.3, f32[128]{0:T(128)S(1)} %get-tuple-element.2), channel_id=1, replica_groups=mesh['dp'=4,'vocab'=8] {'vocab'}, use_global_device_ids=true, to_apply=%region_10.0 | all-reduce | flops 384 | bytes 3072 | tf_op jit(solution)/shard_map/psum | solution.py:41
  549.8 1.1 fusion.1
  550.9 6.5 %psum.31 = f32[]{:T(128)} all-reduce(f32[]{:T(128)} %get-tuple-element.8), channel_id=1, replica_groups=mesh['dp'=4,'vocab'=8] {'dp'}, use_global_device_ids=true, to_apply=%region_12.0 | all-reduce | flops 1 | bytes 8 | tf_op jit(solution)/shard_map/psum | solution.py:52
Async XLA Ops:
  7.2 46.0 %all-gather.5.cloned.1.call-start = ((), (), s32[]{:S(2)}) async-start(), calls=%async_computation.4 | async-start | bytes 1179648 | tf_op jit(solution)/shard_map/all_gather | solution.py:10
  8.9 117.9 %all-gather.3.cloned.1.call-start = ((), (), s32[]{:S(2)}) async-start(), calls=%async_computation.3 | async-start | bytes 4718592 | tf_op jit(solution)/shard_map/all_gather | solution.py:9
  53.1 78.6 %all-to-all-start.1 = ((bf16[128,4,1024]{0,2,1:T(8,128)(2,1)}), bf16[128,4,1024]{0,2,1:T(8,128)(2,1)S(1)}, u32[]{:S(2)}, u32[]{:S(2)}) async-start(bf16[128,4,1024]{0,2,1:T(8,128)(2,1)} %bitcast.17), calls=%async_computation.1 | async-start | bytes 2097152 | tf_op jit(solution)/shard_map/all_to_all | solution.py:21
  131.7 53.1 %all-to-all-start = ((bf16[4,128,4096]{2,1,0:T(8,128)(2,1)}), bf16[4,128,4096]{2,1,0:T(8,128)(2,1)}, u32[]{:S(2)}, u32[]{:S(2)}) async-start(bf16[4,128,4096]{2,1,0:T(8,128)(2,1)} %pad_maximum_fusion.1), calls=%async_computation | async-start | bytes 8388608 | tf_op jit(solution)/shard_map/all_to_all | solution.py:16
  136.6 345.0 %reduce-scatter.2.cloned.1.call-start = ((), (), s32[]{:S(2)}) async-start(), calls=%async_computation.5 | async-start | bytes 41943040 | tf_op jit(solution)/shard_map/reduce_scatter | solution.py:23
Sparse Core Ops, SparseCore 0:
  10.1 42.9 all-gather.4
  55.3 71.4 all-gather.2
  251.7 229.9 reduce-scatter.1
